TPU v7x, 32 devices: a whole 2x2x4 slice. The times are simulated.
32 devices in a mesh: cls: 4 (over y, x), org: 8 (over z, core).
Axes of the slice: x: 2, y: 2, z: 4, core: 2. Of those that a mesh axis runs over, the one named last changes fastest.
Arguments:
- flows_start: float32 [8, 49152], P('cls', 'org'), may hold values from 150 to 300
- interaction: float32 [8, 8, 49152], P('cls', None, 'org'), may hold values from 0.2 to 2
- free_time: float32 [8, 49152], P('cls', 'org'), may hold values from 0.01 to 0.1
- capacity: float32 [49152], P('org'), may hold values from 300 to 900
- demand: int32 [8, 8, 60], P('cls', 'org'), may hold values from 0 to 15
- incidence: int32 [2, 8, 8, 2, 49152], P(None, 'cls', 'org'), may hold values from 0 to 1073741823, as said below
- step_size: float32 [2], replicated, may hold values from 0.3 to 0.6
Outputs:
- flows: float32 [8, 49152], P('cls', 'org')
- costs: float32 [8, 49152], P('cls', 'org')
- skims: float32 [2, 8, 8, 60], P(None, 'cls', 'org')
- gaps: float32 [2], replicated
Inputs may be any that keep to these rules, and one draw needn't show every extreme that they name: Bit b of incidence[k, c, o, w, l] tells whether link l lies on class c's path from anchor o to destination w * 30 + b in iteration k; each path is the union of 4 runs of 64 consecutive links (counted cyclically over the links) at drawn starts, the first of which is shared by all 30 destinations of one word.
All inputs are finite; a program needn't handle non-finite values.
Results may differ from a plain program's by a relative error of at most 0.0013.
Values sent between devices are 32-bit elements; how exact they have to be, the bound alone decides.
A program may use at most 256 MiB of HBM per device.

v0:
```python
import jax
import jax.numpy as jnp
from jax import lax
from jax.sharding import PartitionSpec as P

BITS = 30
ITERS = 2


HIGH = lax.Precision.HIGHEST


def unpack_half(packed):
    shifts = jnp.arange(BITS, dtype=jnp.int32)
    bit_table = jnp.bitwise_and(jnp.right_shift(packed[..., :, None, :], shifts[:, None]), 1)
    new_shape = packed.shape[:-2] + (packed.shape[-2] * BITS, packed.shape[-1])
    return bit_table.reshape(new_shape).astype(jnp.bfloat16)


def link_cost(flows_all, inter, free, cap):
    load_sum = jnp.einsum("cel,el->cl", inter, flows_all, precision=HIGH)
    load_ratio = load_sum / cap
    square = load_ratio * load_ratio
    return free * (1.0 + 0.15 * square * square)


def split_three(values):
    upper = values.astype(jnp.bfloat16)
    remain = values - upper.astype(jnp.float32)
    middle = remain.astype(jnp.bfloat16)
    lowest = (remain - middle.astype(jnp.float32)).astype(jnp.bfloat16)
    return jnp.stack([upper, middle, lowest], axis=1)


def skim_block(bit_table, cost_block):
    parts = split_three(cost_block)
    terms = jnp.einsum("codl,cpl->cpod", bit_table, parts, preferred_element_type=jnp.float32)
    return jnp.sum(terms, axis=1)


def anchor_loads_local(packed_all, trips_half, link_shard, block_count):

    def one_block(block_index):
        word_block = lax.dynamic_slice_in_dim(packed_all, block_index * link_shard, link_shard, 3)
        bit_table = unpack_half(word_block)
        return jnp.einsum("cod,codl->cl", trips_half, bit_table, preferred_element_type=jnp.float32)

    blocks = lax.map(one_block, jnp.arange(block_count, dtype=jnp.int32))
    return jnp.moveaxis(blocks, 0, 1).reshape(blocks.shape[1], block_count * link_shard)


def make_fold(packed_all, link_shard):

    def fold_links(skim_carry, portion, first):
        turn_count = portion.shape[1] // link_shard

        def advance(skim_sum, block_index):
            offset = block_index * link_shard
            word_block = lax.dynamic_slice_in_dim(packed_all, offset, link_shard, 3)
            bit_table = unpack_half(word_block)
            cost_block = lax.dynamic_slice_in_dim(portion, offset, link_shard, 1)
            return (skim_sum + skim_block(bit_table, cost_block), None)

        result, unused = lax.scan(advance, skim_carry, jnp.arange(turn_count, dtype=jnp.int32))
        return result

    return fold_links


def both_totals(cost_part, path_part):
    return lax.psum((cost_part, path_part), ("cls", "org"))


def shards(flows_start, interaction, free_time, capacity, demand, incidence, step_size):
    org_count = lax.axis_size("org")
    link_shard = flows_start.shape[1]
    dest_count = demand.shape[2]
    class_local = demand.shape[0]
    demand_real = demand.astype(jnp.float32)
    trips_half = demand.astype(jnp.bfloat16)
    own_start = lax.axis_index("org") * link_shard
    skim_init = jnp.zeros((class_local, demand.shape[1], dest_count), jnp.float32)
    skim_list = []
    gap_list = []
    inter_full, free_full, cap_full, flow_now = (
        lax.all_gather(interaction, "org", axis=2, tiled=True),
        lax.all_gather(free_time, "org", axis=1, tiled=True),
        lax.all_gather(capacity, "org", axis=0, tiled=True),
        lax.all_gather(flows_start, "org", axis=1, tiled=True),
    )

    def full_cost(flow_value):
        flows_all = lax.all_gather(flow_value, "cls", axis=0, tiled=True)
        return link_cost(flows_all, inter_full, free_full, cap_full)

    for iteration in range(ITERS):
        cost_now = full_cost(flow_now)
        fold_links = make_fold(incidence[iteration], link_shard)
        skim_now = fold_links(skim_init, cost_now, jnp.int32(0))
        partial_value = anchor_loads_local(incidence[iteration], trips_half, link_shard, org_count)
        aon = lax.psum(partial_value, "org")
        product = lax.dynamic_slice_in_dim(cost_now * flow_now, own_start, link_shard, 1)
        cost_total, path_total = both_totals(jnp.sum(product), jnp.sum(demand_real * skim_now))
        gap_list.append((cost_total - path_total) / cost_total)
        skim_list.append(skim_now)
        flow_now = flow_now + step_size[iteration] * (aon - flow_now)
    cost_final = full_cost(flow_now)
    flow_out = lax.dynamic_slice_in_dim(flow_now, own_start, link_shard, 1)
    cost_out = lax.dynamic_slice_in_dim(cost_final, own_start, link_shard, 1)
    return (flow_out, cost_out, jnp.stack(skim_list), jnp.stack(gap_list))


def solution(mesh):
    placed = (
        P("cls", "org"),
        P("cls", None, "org"),
        P("cls", "org"),
        P("org"),
        P("cls", "org", None),
        P(None, "cls", "org", None, None),
        P(),
    )
    return jax.shard_map(
        shards,
        mesh=mesh,
        in_specs=placed,
        out_specs=(P("cls", "org"), P("cls", "org"), P(None, "cls", "org", None), P()),
        check_vma=False,
    )
```

profile of v0, /device:TPU:0, one launch (start us, length us, event | category | flops | bytes accessed | tf_op | source)
XLA Modules:
  0.0 387.4 jit_solution(10713880894416797273)
XLA Ops:
  10.9 32.3 %while.43 = (s32[]{:T(128)}, f32[8,2,6144]{2,1,0:T(2,128)S(1)}, s32[8]{0:T(128)S(1)}, s32[2,1,2,49152]{3,0,2,1:T(2,128)S(1)}, bf16[2,1,60]{2,0,1:T(2,128)(2,1)S(...) while((s32[]{:T(128)}, f32[8,2,6144]{2,1,0:T(2,128)S(1)}, s32[8]{0:T(128)S(1)}, ...), condition=%wide.region_4.5_spmd, body=%wide.region_3.4_spmd.sunk | while | flops 3686406 | bytes 3392847 | solution.py:48
  12.3 1.7 fusion.83
  16.3 1.7 fusion.83
  20.3 1.7 fusion.83
  24.4 1.7 fusion.83
  28.4 1.7 fusion.83
  32.5 1.7 fusion.83
  36.5 1.7 fusion.83
  40.5 1.7 fusion.83
  44.3 32.3 %while.42 = (s32[]{:T(128)}, f32[8,2,6144]{2,1,0:T(2,128)S(1)}, s32[8]{0:T(128)S(1)}, s32[2,1,2,49152]{3,0,2,1:T(2,128)S(1)}, bf16[2,1,60]{2,0,1:T(2,128)(2,1)S(...) while((s32[]{:T(128)}, f32[8,2,6144]{2,1,0:T(2,128)S(1)}, s32[8]{0:T(128)S(1)}, ...), condition=%wide.region_1.0_spmd, body=%wide.region_0.1_spmd.sunk | while | flops 3686406 | bytes 3392847 | solution.py:48
  77.5 17.5 %all_gather.21 = f32[2,49152]{1,0:T(2,128)} all-gather(f32[2,6144]{1,0:T(2,128)S(1)} %copy-done.7), channel_id=1, replica_groups=mesh['cls'=4,'org'=8] {'org'}, dimensions={1}, use_global_device_ids=true | all-gather | bytes 442368 | tf_op jit(solution)/shard_map/all_gather | solution.py:89
  95.7 42.7 %all-reduce.4.cloned.1.call-done = (f32[2,49152]{1,0:T(2,128)}, f32[2,49152]{1,0:T(2,128)}) async-done(((f32[2,49152]{1,0:T(2,128)}, f32[2,49152]{1,0:T(2,128)}), (f32[2,49152]{1,0:T(2,128)}, f32[2,49152]{1,0:T(2,128)})) %all-reduce.4.cloned.1.call-update) | async-done | bytes 786448 | tf_op jit(solution)/shard_map/psum | solution.py:101
  138.4 3.8 multiply_add_fusion
  143.5 15.2 %all_gather.25 = f32[49152]{0:T(1024)} all-gather(f32[6144]{0:T(1024)S(1)} %copy-done.9), channel_id=1, replica_groups=mesh['cls'=4,'org'=8] {'org'}, dimensions={0}, use_global_device_ids=true | all-gather | bytes 221184 | tf_op jit(solution)/shard_map/all_gather | solution.py:88
  158.7 14.7 %all_gather.22 = f32[2,49152]{1,0:T(2,128)S(1)} all-gather(f32[2,6144]{1,0:T(2,128)S(1)} %copy-done.8), channel_id=1, replica_groups=mesh['cls'=4,'org'=8] {'org'}, dimensions={1}, use_global_device_ids=true | all-gather | bytes 442368 | tf_op jit(solution)/shard_map/all_gather | solution.py:87
  174.8 2.5 reshape.94
  177.3 2.5 reshape.92
  179.8 24.8 %all-gather.14.cloned.1.call-done = f32[4,2,49152]{2,1,0:T(2,128)} async-done(((f32[1,2,49152]{2,1,0:T(2,128)}), f32[4,2,49152]{2,1,0:T(2,128)}) %all-gather.14.cloned.1.call-update) | async-done | bytes 1572880 | tf_op jit(solution)/shard_map/all_gather | solution.py:93
  204.6 3.6 reshape.96
  208.2 36.0 %all-gather.8.cloned.1.call-done = f32[2,8,49152]{2,1,0:T(8,128)} async-done(((f32[2,8,6144]{2,1,0:T(8,128)}), f32[2,8,49152]{2,1,0:T(8,128)}) %all-gather.8.cloned.1.call-update) | async-done | bytes 3145744 | tf_op jit(solution)/shard_map/all_gather | solution.py:86
  244.2 6.9 %multiply_reduce_fusion.1 = (f32[49152,2]{0,1:T(2,128)S(1)}, f32[49152,2]{0,1:T(2,128)S(1)}, f32[49152,2]{0,1:T(2,128)}) fusion(f32[2,8,49152]{2,1,0:T(8,128)} %all-gather.8.cloned.1.call-done, f32[49152,8]{0,1:T(8,128)S(1)} %bitcast.155, f32[49152,8]{0,1:T(8,128)} %bitcast.157, f32[49152,8]{0,1:T(8,128)S(1)} %bitcast.156), kind=kLoop, calls=%fused_computation.59 | loop fusion | flops 4423680 | bytes 9043968 | tf_op jit(solution)/shard_map/cel,el->cl/dot_general | solution.py:21
  253.4 39.4 %while.44 = (s32[]{:T(128)}, f32[2,1,60]{2,0,1:T(2,128)S(1)}, s32[8]{0:T(128)S(1)}, f32[2,49152]{1,0:T(2,128)S(1)}, s32[2,1,2,49152]{3,0,2,1:T(2,128)}, /*index=5*/s32[]{:T(128)}, s32[1]{0:T(128)}, s32[]{:T(128)}, s32[]{:T(128)}) while((s32[]{:T(128)}, f32[2,1,60]{2,0,1:T(2,128)S(1)}, s32[8]{0:T(128)S(1)}, ...), condition=%wide.region_8.9_spmd.clone, body=%wide.region_6.8_spmd.clone.sunk | while | flops 6943207 | bytes 3615725 | solution.py:64
  294.2 39.4 %while.45 = (s32[]{:T(128)}, f32[2,1,60]{2,0,1:T(2,128)S(1)}, s32[8]{0:T(128)S(1)}, f32[2,49152]{1,0:T(2,128)S(1)}, s32[2,1,2,49152]{3,0,2,1:T(2,128)}, /*index=5*/s32[]{:T(128)}, s32[1]{0:T(128)}, s32[]{:T(128)}, s32[]{:T(128)}) while((s32[]{:T(128)}, f32[2,1,60]{2,0,1:T(2,128)S(1)}, s32[8]{0:T(128)S(1)}, ...), condition=%wide.region_11.12_spmd.clone, body=%wide.region_9.11_spmd.clone.sunk | while | flops 6943207 | bytes 3615725 | solution.py:64
  334.2 39.7 %all-reduce = (f32[]{:T(128)}, f32[]{:T(128)}, f32[]{:T(128)}, f32[]{:T(128)}) all-reduce(f32[]{:T(128)} %fusion.53, f32[]{:T(128)} %get-tuple-element.186, f32[]{:T(128)} %fusion.54, f32[]{:T(128)} %get-tuple-element.185), channel_id=1, replica_groups=mesh['cls'=4,'org'=8] {'cls','org'}, use_global_device_ids=true, to_apply=%region_17.18 | all-reduce | flops 4 | bytes 32 | tf_op jit(solution)/shard_map/psum | solution.py:71
  (353 shorter events, 121.2 us)
Async XLA Ops:
  8.0 130.4 %all-reduce.4.cloned.1.call-start = ((), (), s32[]{:S(2)}) async-start(), calls=%async_computation.4 | async-start | bytes 1572864 | tf_op jit(solution)/shard_map/psum | solution.py:101
  8.0 1.5 copy-start.11
  43.2 1.0 copy-start
  43.2 1.1 copy-start.6
  43.3 34.1 %copy-start.7 = (f32[2,6144]{1,0:T(2,128)S(1)}, f32[2,6144]{1,0:T(2,128)}, u32[]{:S(2)}) copy-start(f32[2,6144]{1,0:T(2,128)} %param.15) | copy-start | bytes 147460
  76.6 0.8 copy-start.5
  76.6 65.5 %copy-start.1 = (s32[2,1,2,49152]{3,0,2,1:T(2,128)}, s32[2,1,2,49152]{3,0,2,1:T(2,128)S(1)}, u32[]{:S(2)}) copy-start(s32[2,1,2,49152]{3,0,2,1:T(2,128)S(1)} %get-tuple-element.496) | copy-start | bytes 2359300
  76.6 18.4 %copy-start.10 = (f32[2]{0:T(128)S(1)}, f32[2]{0:T(128)}, u32[]{:S(2)}) copy-start(f32[2]{0:T(128)} %param.21) | copy-start | bytes 28
  77.4 97.4 %all-gather.12.cloned.1.call-start = ((), (), s32[]{:S(2)}) async-start(), calls=%async_computation.2 | async-start | bytes 1966080 | tf_op jit(solution)/shard_map/all_gather | solution.py:93
  95.0 82.3 %all-gather.10.cloned.1.call-start = ((), (), s32[]{:S(2)}) async-start(), calls=%async_computation.1 | async-start | bytes 1966080 | tf_op jit(solution)/shard_map/all_gather | solution.py:93
  138.4 5.1 %copy-start.9 = (f32[6144]{0:T(1024)S(1)}, f32[6144]{0:T(1024)}, u32[]{:S(2)}) copy-start(f32[6144]{0:T(1024)} %param.18) | copy-start | bytes 73732
  138.4 20.3 %copy-start.8 = (f32[2,6144]{1,0:T(2,128)S(1)}, f32[2,6144]{1,0:T(2,128)}, u32[]{:S(2)}) copy-start(f32[2,6144]{1,0:T(2,128)} %param.17) | copy-start | bytes 147460
  142.2 62.4 %all-gather.14.cloned.1.call-start = ((), (), s32[]{:S(2)}) async-start(), calls=%async_computation.3 | async-start | bytes 1966080 | tf_op jit(solution)/shard_map/all_gather | solution.py:93
  142.8 101.5 %all-gather.8.cloned.1.call-start = ((), (), s32[]{:S(2)}) async-start(), calls=%async_computation | async-start | bytes 3538944 | tf_op jit(solution)/shard_map/all_gather | solution.py:86
  244.2 6.9 %copy-start.2 = (f32[49152]{0:T(1024)S(1)}, f32[49152]{0:T(1024)}, u32[]{:S(2)}) copy-start(f32[49152]{0:T(1024)} %all_gather.25) | copy-start | bytes 589828
  294.2 83.5 %copy-start.3 = (f32[49152]{0:T(1024)S(1)}, f32[49152]{0:T(1024)}, u32[]{:S(2)}) copy-start(f32[49152]{0:T(1024)} %all_gather.25) | copy-start | bytes 589828
  294.2 83.5 %copy-start.4 = (f32[49152,2]{0,1:T(2,128)S(1)}, f32[49152,2]{0,1:T(2,128)}, u32[]{:S(2)}) copy-start(f32[49152,2]{0,1:T(2,128)} %get-tuple-element.184) | copy-start | bytes 1179652
Sparse Core Ops, SparseCore 0:
  77.5 60.7 all-reduce.3
Sparse Core Ops, SparseCore 1:
  95.1 31.7 all-gather.11
  142.3 29.8 all-gather.9
  173.8 30.7 all-gather.13
  206.2 38.0 all-gather.7
where the time goes:
time: 389 us; the launch traced here: 387 us
  waiting for transfers between devices  105 us (27%)
  blocking collectives  87 us (22%)
  other arithmetic  73.1 us (19%)
  local copies, waits for them, and re-layouts  54.5 us (14%)
  matrix products  25.3 us (7%)
  loops' own time  22.7 us (6%)
  between operations  19.7 us (5%)
    convert_element_type x32, other arithmetic, unpack_half(): return bit_table.reshape(new_shape).astype(jnp.bfloat16)  55.2 us
    psum x1, waiting for transfers between devices, shards(): aon = lax.psum(partial_value, 'org')  42.7 us
    psum x1, blocking collectives, both_totals(): return lax.psum((cost_part, path_part), ('cls', 'org'))  39.7 us
    all_gather x1, waiting for transfers between devices, shards(): lax.all_gather(interaction, 'org', axis=2, tiled=True)  36 us
    all_gather x3, waiting for transfers between devices, full_cost(): flows_all = lax.all_gather(flow_value, 'cls', axis=0, tiled=True)  24.8 us
    dynamic_slice x32, local copies, waits for them, and re-layouts, fold_links(): lax.scan(advance, skim_carry, jnp.arange(turn_count, dtype=jnp.int32))  18.8 us
    all_gather x1, blocking collectives, shards(): lax.all_gather(flows_start, 'org', axis=1, tiled=True)  17.5 us
    shift_right_arithmetic x96, local copies, waits for them, and re-layouts, unpack_half(): jnp.right_shift(packed[..., :, None, :], shifts[:, None])  17.5 us
  transfers between devices with their start and end apart: 5, of which 3 were waited for; matrix products, arithmetic and copies ran while one was open for 4% of the time, Pallas kernels for 0%

commit v1 on v0

v1 whole, which is shorter than its diff:
```python
import functools

import jax
import jax.numpy as jnp
from jax import lax
from jax.experimental import pallas as pl
from jax.experimental.pallas import tpu as pltpu
from jax.sharding import PartitionSpec as P

BITS = 30
TRIP_BITS = 4
LANES = 128
SUB = 8
MESH = pl.DeviceIdType.MESH


def kernel(
    n_cls, n_org, iters, class_local, words, link_rows,
    flow_ref, inter_ref, free_ref, cap_ref, demand_ref, inc_ref, step_ref,
    flow_out, cost_out, skim_out, gap_out,
    flows_all, aon_own, aon_pair, pair_buf, rs_buf, aon_total, times, acc, part_one, part_two,
    flow_send, flow_recv, pair_send, pair_recv, rs_send, rs_recv,
    time_send, time_recv, fwd_send, fwd_recv, one_send, one_recv, two_send, two_recv,
):
    half = n_org // 2
    my_cls = lax.axis_index("cls")
    my_org = lax.axis_index("org")
    my_z = my_org // 2
    core = my_org % 2
    other = 1 - core
    partner = my_z * 2 + other
    groups = link_rows // SUB
    class_count = n_cls * class_local

    barrier = pltpu.get_barrier_semaphore()
    for i in range(1, n_org):
        pl.semaphore_signal(barrier, inc=1, device_id={"org": (my_org + i) % n_org}, device_id_type=MESH)
    for i in range(1, n_cls):
        pl.semaphore_signal(barrier, inc=1, device_id={"cls": (my_cls + i) % n_cls}, device_id_type=MESH)

    demand = demand_ref[...]
    lane = lax.broadcasted_iota(jnp.int32, demand.shape, 1)
    spot = lane % BITS
    low_half = BITS // 2
    masks = {}
    for bit in range(TRIP_BITS):
        chosen = jnp.bitwise_and(jnp.right_shift(demand, bit), 1)
        for w in range(words):
            inside = lane // BITS == w
            low = jnp.where(inside & (spot < low_half), jnp.left_shift(chosen, spot % low_half), 0)
            high = jnp.where(inside & (spot >= low_half), jnp.left_shift(chosen, spot % low_half), 0)
            low_sum = jnp.sum(low.astype(jnp.float32), axis=1, keepdims=True).astype(jnp.int32)
            high_sum = jnp.sum(high.astype(jnp.float32), axis=1, keepdims=True).astype(jnp.int32)
            both = low_sum + jnp.left_shift(high_sum, low_half)
            for c in range(class_local):
                masks[bit, w, c] = jnp.broadcast_to(both[c:c + 1, :], (SUB, LANES))

    def aon_chunks(k, parity, dest):
        def one(j, carry):
            target = 2 * ((my_z + j) % half) + parity
            base = target * (link_rows * words)
            for c in range(class_local):
                for g in range(groups):
                    word = [
                        inc_ref[k, c, pl.ds(base + g * SUB * words + w, SUB, stride=words), :]
                        for w in range(words)
                    ]
                    total = None
                    for bit in range(TRIP_BITS):
                        count = None
                        for w in range(words):
                            ones = lax.population_count(jnp.bitwise_and(word[w], masks[bit, w, c]))
                            count = ones if count is None else count + ones
                        count = jnp.left_shift(count, bit)
                        total = count if total is None else total + count
                    dest[k, j, c, g * SUB:(g + 1) * SUB, :] = total.astype(jnp.float32)
            return carry

        lax.fori_loop(0, half, one, 0)

    def copy(src, dst, send, recv, device):
        made = pltpu.make_async_remote_copy(
            src_ref=src, dst_ref=dst, send_sem=send, recv_sem=recv, device_id=device, device_id_type=MESH
        )
        made.start()
        return made

    def pair_copy(k):
        return copy(aon_pair.at[k], pair_buf.at[k], pair_send.at[k], pair_recv.at[k], {"org": partner})

    def flow_copies(k, src):
        return [
            copy(src, flows_all.at[k, my_cls], flow_send.at[k, i], flow_recv.at[k, i], {"cls": (my_cls + i) % n_cls})
            for i in range(1, n_cls)
        ]

    def rs_copies(k):
        return [
            copy(aon_own.at[k, j], rs_buf.at[k, j], rs_send.at[k, j], rs_recv.at[k, j],
                 {"org": 2 * ((my_z + j) % half) + core})
            for j in range(1, half)
        ]

    def time_copies(k):
        made = [copy(times.at[k, 0, 0], times.at[k, 0, 1], time_send.at[k, 0], time_recv.at[k, 0], {"org": partner})]
        for j in range(1, half):
            made.append(
                copy(times.at[k, 0, 0], times.at[k, j, 0], time_send.at[k, j], time_recv.at[k, j],
                     {"org": 2 * ((my_z + j) % half) + core})
            )
        return made

    def forward(k, j):
        return copy(times.at[k, j, 0], times.at[k, j, 1], fwd_send.at[k, j], fwd_recv.at[k, j], {"org": partner})

    def flow_of(k, c):
        return flows_all[k, my_cls, pl.ds(c, link_rows, stride=class_local), :]

    def link_time(k, c):
        load = None
        for e in range(class_count):
            weight = inter_ref[c, pl.ds(e, link_rows, stride=class_count), :]
            flow = flows_all[k, e // class_local, pl.ds(e % class_local, link_rows, stride=class_local), :]
            term = weight * flow
            load = term if load is None else load + term
        ratio = load / cap_ref[...]
        square = ratio * ratio
        return free_ref[pl.ds(c, link_rows, stride=class_local), :] * (1.0 + 0.15 * square * square)

    def fold_rows(value):
        return jnp.sum(value.reshape(groups, SUB, LANES), axis=0)

    def skim_chunk(k, j, p, first):
        source = 2 * ((my_z + half - j) % half) + (core if p == 0 else other)
        base = source * (link_rows * words)
        for c in range(class_local):
            cost = [times[k, j, p, c, g * SUB:(g + 1) * SUB, :] for g in range(groups)]
            for w in range(words):
                word = [
                    inc_ref[k, c, pl.ds(base + g * SUB * words + w, SUB, stride=words), :] for g in range(groups)
                ]
                for b in range(BITS):
                    total = None
                    for g in range(groups):
                        term = jnp.where(jnp.bitwise_and(word[g], 1 << b) != 0, cost[g], 0.0)
                        total = term if total is None else total + term
                    row = (w * BITS + b) * SUB
                    if first:
                        acc[k, c, row:row + SUB, :] = total
                    else:
                        acc[k, c, row:row + SUB, :] += total

    def skim_finish(k):
        count = words * BITS
        ones = jnp.ones((SUB, LANES), jnp.float32)
        for c in range(class_local):
            rows = None
            for s in range(SUB):
                value = acc[k, c, pl.ds(s, count, stride=SUB), :]
                rows = value if rows is None else rows + value
            summed = lax.dot_general(
                ones, rows, (((1,), (1,)), ((), ())),
                precision=lax.Precision.HIGHEST, preferred_element_type=jnp.float32,
            )
            skim_out[k, c:c + 1, :] = summed[0:1, :]

    def reduce_pair(k):
        aon_own[k] = aon_own[k] + pair_buf[k]

    def aon_sum(k):
        total = aon_own[k, 0]
        for j in range(1, half):
            total = total + rs_buf[k, j]
        aon_total[k] = total

    def next_flow(k):
        step = step_ref[k]
        for c in range(class_local):
            now = flow_of(k, c)
            flows_all[k + 1, my_cls, pl.ds(c, link_rows, stride=class_local), :] = now + step * (aon_total[k, c] - now)

    def partials(k):
        cost = path = None
        for c in range(class_local):
            value = times[k, 0, 0, c]
            a, b = fold_rows(value * flow_of(k, c)), fold_rows(value * aon_total[k, c])
            cost = a if cost is None else cost + a
            path = b if path is None else path + b
        part_one[my_cls, 2 * k] = cost
        part_one[my_cls, 2 * k + 1] = path

    flows_all[0, my_cls] = flow_ref[...]
    aon_chunks(0, other, aon_pair)
    pl.semaphore_wait(barrier, n_org - 1 + n_cls - 1)
    pair0 = pair_copy(0)
    flow0 = flow_copies(0, flow_ref)
    aon_chunks(0, core, aon_own)
    pair0.wait()
    reduce_pair(0)
    rs0 = rs_copies(0)
    for made in flow0:
        made.wait()
    for c in range(class_local):
        times[0, 0, 0, c] = link_time(0, c)
    time0 = time_copies(0)
    aon_chunks(1, other, aon_pair)
    pair1 = pair_copy(1)
    aon_chunks(1, core, aon_own)
    pair1.wait()
    reduce_pair(1)
    rs1 = rs_copies(1)
    skim_chunk(0, 0, 0, True)
    for made in rs0:
        made.wait()
    aon_sum(0)
    next_flow(0)
    flow1 = flow_copies(1, flows_all.at[1, my_cls])
    time0[0].wait()
    forward0 = []
    for j in range(1, half):
        time0[j].wait()
        forward0.append(forward(0, j))
    skim_chunk(0, 0, 1, False)
    for j in range(1, half):
        skim_chunk(0, j, 0, False)
    for made in flow1:
        made.wait()
    for c in range(class_local):
        times[1, 0, 0, c] = link_time(1, c)
    time1 = time_copies(1)
    for made in rs1:
        made.wait()
    aon_sum(1)
    next_flow(1)
    flow2 = flow_copies(2, flows_all.at[2, my_cls])
    partials(0)
    partials(1)
    first_sums = [
        copy(part_one.at[my_cls], part_one.at[my_cls], one_send.at[i], one_recv.at[i], {"cls": (my_cls + i) % n_cls})
        for i in range(1, n_cls)
    ]
    flow_out[...] = flows_all[2, my_cls]
    for j in range(1, half):
        forward0[j - 1].wait()
        skim_chunk(0, j, 1, False)
    skim_finish(0)
    skim_chunk(1, 0, 0, True)
    time1[0].wait()
    forward1 = []
    for j in range(1, half):
        time1[j].wait()
        forward1.append(forward(1, j))
    for made in first_sums:
        made.wait()
    total = part_one[0]
    for i in range(1, n_cls):
        total = total + part_one[i]
    part_two[my_org] = total
    second_sums = [
        copy(part_two.at[my_org], part_two.at[my_org], two_send.at[i], two_recv.at[i], {"org": (my_org + i) % n_org})
        for i in range(1, n_org)
    ]
    skim_chunk(1, 0, 1, False)
    for j in range(1, half):
        skim_chunk(1, j, 0, False)
    for made in flow2:
        made.wait()
    for c in range(class_local):
        cost_out[pl.ds(c, link_rows, stride=class_local), :] = link_time(2, c)
    for j in range(1, half):
        forward1[j - 1].wait()
        skim_chunk(1, j, 1, False)
    skim_finish(1)
    for made in second_sums:
        made.wait()
    total = part_two[0]
    for i in range(1, n_org):
        total = total + part_two[i]
    lanes_out = lax.broadcasted_iota(jnp.int32, (1, LANES), 1)
    gaps = jnp.zeros((1, LANES), jnp.float32)
    for k in range(iters):
        cost = jnp.sum(jnp.sum(total[2 * k], axis=0, keepdims=True), axis=1, keepdims=True)
        path = jnp.sum(jnp.sum(total[2 * k + 1], axis=0, keepdims=True), axis=1, keepdims=True)
        gaps = jnp.where(lanes_out == k, (cost - path) / cost, gaps)
    gap_out[...] = gaps[:, :iters]


def shards(n_cls, n_org, flows_start, interaction, free_time, capacity, demand, incidence, step_size):
    class_local, link_shard = flows_start.shape
    class_count = interaction.shape[1]
    iters, _, anchors, words, links = incidence.shape
    assert iters == 2 and anchors == 1 and class_count == n_cls * class_local
    link_rows = link_shard // LANES
    half = n_org // 2

    def interleave(x):
        lead = x.shape[:-2]
        rows, cols = x.shape[-2:]
        x = x.reshape(lead + (rows, cols // LANES, LANES))
        return jnp.swapaxes(x, -3, -2).reshape(lead + (rows * cols // LANES, LANES))

    def restore(x):
        x = x.reshape(link_rows, class_local, LANES)
        return jnp.swapaxes(x, 0, 1).reshape(class_local, link_shard)

    inc = interleave(incidence.reshape(iters, class_local, words, links))
    vmem = pl.BlockSpec(memory_space=pltpu.VMEM)
    smem = pl.BlockSpec(memory_space=pltpu.SMEM)
    f32 = jnp.float32
    tile = (class_local, link_rows, LANES)
    dma = pltpu.SemaphoreType.DMA
    count = demand.shape[2]
    outs = pl.pallas_call(
        functools.partial(kernel, n_cls, n_org, iters, class_local, words, link_rows),
        out_shape=(
            jax.ShapeDtypeStruct((class_local * link_rows, LANES), f32),
            jax.ShapeDtypeStruct((class_local * link_rows, LANES), f32),
            jax.ShapeDtypeStruct((iters, class_local, count), f32),
            jax.ShapeDtypeStruct((1, iters), f32),
        ),
        in_specs=[vmem] * 6 + [smem],
        out_specs=(vmem,) * 4,
        scratch_shapes=[
            pltpu.VMEM((iters + 1, n_cls, class_local * link_rows, LANES), f32),
            pltpu.VMEM((iters, half) + tile, f32),
            pltpu.VMEM((iters, half) + tile, f32),
            pltpu.VMEM((iters, half) + tile, f32),
            pltpu.VMEM((iters, half) + tile, f32),
            pltpu.VMEM((iters,) + tile, f32),
            pltpu.VMEM((iters, half, 2) + tile, f32),
            pltpu.VMEM((iters, class_local, words * BITS * SUB, LANES), f32),
            pltpu.VMEM((n_cls, 2 * iters, SUB, LANES), f32),
            pltpu.VMEM((n_org, 2 * iters, SUB, LANES), f32),
            dma((iters + 1, n_cls)), dma((iters + 1, n_cls)),
            dma((iters,)), dma((iters,)),
            dma((iters, half)), dma((iters, half)),
            dma((iters, half)), dma((iters, half)),
            dma((iters, half)), dma((iters, half)),
            dma((n_cls,)), dma((n_cls,)),
            dma((n_org,)), dma((n_org,)),
        ],
        compiler_params=pltpu.CompilerParams(collective_id=0, has_side_effects=True),
    )(
        interleave(flows_start), interleave(interaction), interleave(free_time),
        capacity.reshape(link_rows, LANES), demand.reshape(class_local, count), inc, step_size,
    )
    flows, costs, skims, gaps = outs
    return restore(flows), restore(costs), skims.reshape(iters, class_local, anchors, count), gaps.reshape(iters)


def solution(mesh):
    placed = (
        P("cls", "org"),
        P("cls", None, "org"),
        P("cls", "org"),
        P("org"),
        P("cls", "org", None),
        P(None, "cls", "org", None, None),
        P(),
    )
    return jax.shard_map(
        functools.partial(shards, mesh.shape["cls"], mesh.shape["org"]),
        mesh=mesh,
        in_specs=placed,
        out_specs=(P("cls", "org"), P("cls", "org"), P(None, "cls", "org", None), P()),
        check_vma=False,
    )
```

time: 389 us -> 40.4 us (0.10)
  waiting for transfers between devices: 105 us -> 0 us
  blocking collectives: 87 us -> 0 us
  other arithmetic: 73.1 us -> 0 us
  local copies, waits for them, and re-layouts: 54.5 us -> 5.21 us
  Pallas kernels: 0 us -> 34.2 us
  matrix products: 25.3 us -> 0 us
  loops' own time: 22.7 us -> 0 us
  between operations: 19.7 us -> 0.64 us
    all_gather x4 -> x0, waiting for transfers between devices: 60.8 us -> none  [the longest x1 36 us: shards(): lax.all_gather(interaction, 'org', axis=2, tiled=True)]
    convert_element_type x33 -> x0, other arithmetic: 55.2 us -> none  [the longest x32 55.2 us: unpack_half(): return bit_table.reshape(new_shape).astype(jnp.bfloat16)]
    all_gather x3 -> x0, blocking collectives: 47.3 us -> none  [the longest x1 17.5 us: shards(): lax.all_gather(flows_start, 'org', axis=1, tiled=True)]
    psum x1 -> x0, waiting for transfers between devices: 42.7 us -> none  [shards(): aon = lax.psum(partial_value, 'org')]
    psum x1 -> x0, blocking collectives: 39.7 us -> none  [both_totals(): return lax.psum((cost_part, path_part), ('cls', 'org'))]
    pallas_call x0 -> x1, Pallas kernels: none -> 34.2 us  [shards(): pl.pallas_call(functools.partial(kernel, n_cls, n_org, iters, class_local...]
    dot_general x32 -> x0, matrix products: 25.3 us -> none  [the longest x16 14.3 us: one_block(): jnp.einsum('cod,codl->cl', trips_half, bit_table, preferred_element_type=...]
    another operation x4 -> x0, loops' own time: 22.7 us -> none  [the longest x2 11.6 us: fold_links(): lax.scan(advance, skim_carry, jnp.arange(turn_count, dtype=jnp.int32))]
  transfers between devices with their start and end apart: 5 -> 0, of which waited for: 3 -> 0; matrix products, arithmetic and copies ran while one was open for 4% -> 0% of each run, Pallas kernels for 0% -> 0%
where the time goes in v1:
time: 40.4 us; the launch traced here: 40.1 us
  Pallas kernels  34.2 us (85%)
  local copies, waits for them, and re-layouts  5.21 us (13%)
  between operations  0.64 us (2%)
    pallas_call x1, Pallas kernels, shards(): pl.pallas_call(functools.partial(kernel, n_cls, n_org, iters, class_local...  34.2 us
    unnamed x4, local copies, waits for them, and re-layouts  5.21 us

profile of v1, /device:TPU:0, one launch (start us, length us, event | category | flops | bytes accessed | tf_op | source)
XLA Modules:
  0.0 40.1 jit_solution(4406631979372326247)
XLA Ops:
  0.6 34.2 %shard_map.102 = (f32[96,128]{1,0:T(8,128)}, f32[96,128]{1,0:T(8,128)}, f32[2,2,60]{2,1,0:T(2,128)}, f32[1,2]{1,0:T(1,128)}) custom-call(f32[96,128]{1,0:T(8,128)} %bitcast.40, f32[2,384,128]{2,1,0:T(8,128)} %bitcast.37, f32[96,128]{1,0:T(8,128)} %bitcast.41, f32[48,128]{1,0:T(8,128)} %bitcast.42, s32[2,60]{1,0:T(2,128)} %bitcast.44, ...), custom_call_target="tpu_custom_call" | custom-call | tf_op jit(solution)/shard_map/pallas_call | solution.py:313
  34.8 1.4 %copy.21 = f32[2,6144]{1,0:T(2,128)} copy(f32[2,6144]{1,0:T(2,128)} %bitcast.39) | data formatting | bytes 98304
  36.3 1.4 %copy.22 = f32[2,6144]{1,0:T(2,128)} copy(f32[2,6144]{1,0:T(2,128)} %bitcast.38) | data formatting | bytes 98304
  37.7 1.3 %copy.23 = f32[2,2,1,60]{3,2,1,0:T(1,128)} copy(f32[2,2,1,60]{3,2,1,0:T(1,128)} %bitcast.43) | data formatting | bytes 1920
  39.0 1.1 %copy.24 = f32[2]{0:T(128)} copy(f32[2]{0:T(128)} %bitcast.45) | data formatting | bytes 16

commit v2 on v1

--- a/solution.py
+++ b/solution.py
@@ -16,21 +16,30 @@
 
 def kernel(
     n_cls, n_org, iters, class_local, words, link_rows,
-    flow_ref, inter_ref, free_ref, cap_ref, demand_ref, inc_ref, step_ref,
+    flow_ref, inter_hbm, free_ref, cap_ref, demand_ref, inc_hbm, step_ref,
     flow_out, cost_out, skim_out, gap_out,
-    flows_all, aon_own, aon_pair, pair_buf, rs_buf, aon_total, times, acc, part_one, part_two,
-    flow_send, flow_recv, pair_send, pair_recv, rs_send, rs_recv,
-    time_send, time_recv, fwd_send, fwd_recv, one_send, one_recv, two_send, two_recv,
+    inc_ref, inter_ref, flows_all, aon, aon_recv, times, acc, part_one, part_two,
+    inc_sem, inter_sem, flow_send, flow_recv, pair_send, pair_recv, rs_send, rs_recv,
+    time_send, time_recv, one_send, one_recv, two_send, two_recv,
 ):
-    half = n_org // 2
     my_cls = lax.axis_index("cls")
     my_org = lax.axis_index("org")
-    my_z = my_org // 2
-    core = my_org % 2
-    other = 1 - core
-    partner = my_z * 2 + other
     groups = link_rows // SUB
     class_count = n_cls * class_local
+    levels = [1 << i for i in range(n_org.bit_length() - 1)]
+
+    def across(mask):
+        place = my_org
+        for level in levels:
+            if mask & level:
+                place = place + level * (1 - 2 * ((my_org // level) % 2))
+        return place
+
+    loads = [pltpu.make_async_copy(inc_hbm.at[k], inc_ref.at[k], inc_sem.at[k]) for k in range(iters)]
+    inter_load = pltpu.make_async_copy(inter_hbm, inter_ref, inter_sem)
+    loads[0].start()
+    loads[1].start()
+    inter_load.start()
 
     barrier = pltpu.get_barrier_semaphore()
     for i in range(1, n_org):
@@ -55,10 +64,17 @@
             for c in range(class_local):
                 masks[bit, w, c] = jnp.broadcast_to(both[c:c + 1, :], (SUB, LANES))
 
-    def aon_chunks(k, parity, dest):
-        def one(j, carry):
-            target = 2 * ((my_z + j) % half) + parity
-            base = target * (link_rows * words)
+    def aon_chunks(k, parity):
+        core = my_org % 2
+        place = core + parity * (1 - 2 * core)
+
+        def one(h, carry):
+            upper = 0
+            for level in levels[1:]:
+                mine = (my_org // level) % 2
+                wanted = (h // (level // 2)) % 2
+                upper = upper + level * ((mine + wanted) % 2)
+            base = (upper + place) * (link_rows * words)
             for c in range(class_local):
                 for g in range(groups):
                     word = [
@@ -73,10 +89,10 @@
                             count = ones if count is None else count + ones
                         count = jnp.left_shift(count, bit)
                         total = count if total is None else total + count
-                    dest[k, j, c, g * SUB:(g + 1) * SUB, :] = total.astype(jnp.float32)
+                    aon[k, parity, h, c, g * SUB:(g + 1) * SUB, :] = total.astype(jnp.float32)
             return carry
 
-        lax.fori_loop(0, half, one, 0)
+        lax.fori_loop(0, n_org // 2, one, 0)
 
     def copy(src, dst, send, recv, device):
         made = pltpu.make_async_remote_copy(
@@ -86,32 +102,32 @@
         return made
 
     def pair_copy(k):
-        return copy(aon_pair.at[k], pair_buf.at[k], pair_send.at[k], pair_recv.at[k], {"org": partner})
+        return copy(aon.at[k, 1], aon_recv.at[k, 1], pair_send.at[k], pair_recv.at[k], {"org": across(1)})
+
+    def load_send(k, r):
+        level = r & -r
+        return copy(aon.at[k, 0, r // 2], aon_recv.at[k, 0, r // 2], rs_send.at[k, r], rs_recv.at[k, r],
+                    {"org": across(level)})
+
+    def load_join(k, r):
+        held = r - (r & -r)
+        aon[k, 0, held // 2] += aon_recv[k, 0, r // 2]
+
+    def time_sends(k, m):
+        sent = {}
+        low = (m & -m) if m else n_org
+        for level in reversed(levels):
+            if level < low:
+                to = m + level
+                sent[to] = copy(times.at[k, m], times.at[k, to], time_send.at[k, to], time_recv.at[k, to],
+                                {"org": across(level)})
+        return sent
 
     def flow_copies(k, src):
         return [
             copy(src, flows_all.at[k, my_cls], flow_send.at[k, i], flow_recv.at[k, i], {"cls": (my_cls + i) % n_cls})
             for i in range(1, n_cls)
         ]
-
-    def rs_copies(k):
-        return [
-            copy(aon_own.at[k, j], rs_buf.at[k, j], rs_send.at[k, j], rs_recv.at[k, j],
-                 {"org": 2 * ((my_z + j) % half) + core})
-            for j in range(1, half)
-        ]
-
-    def time_copies(k):
-        made = [copy(times.at[k, 0, 0], times.at[k, 0, 1], time_send.at[k, 0], time_recv.at[k, 0], {"org": partner})]
-        for j in range(1, half):
-            made.append(
-                copy(times.at[k, 0, 0], times.at[k, j, 0], time_send.at[k, j], time_recv.at[k, j],
-                     {"org": 2 * ((my_z + j) % half) + core})
-            )
-        return made
-
-    def forward(k, j):
-        return copy(times.at[k, j, 0], times.at[k, j, 1], fwd_send.at[k, j], fwd_recv.at[k, j], {"org": partner})
 
     def flow_of(k, c):
         return flows_all[k, my_cls, pl.ds(c, link_rows, stride=class_local), :]
@@ -130,11 +146,11 @@
     def fold_rows(value):
         return jnp.sum(value.reshape(groups, SUB, LANES), axis=0)
 
-    def skim_chunk(k, j, p, first):
-        source = 2 * ((my_z + half - j) % half) + (core if p == 0 else other)
-        base = source * (link_rows * words)
+    def skim_chunk(k, m):
+        first = m == 0
+        base = across(m) * (link_rows * words)
         for c in range(class_local):
-            cost = [times[k, j, p, c, g * SUB:(g + 1) * SUB, :] for g in range(groups)]
+            cost = [times[k, m, c, g * SUB:(g + 1) * SUB, :] for g in range(groups)]
             for w in range(words):
                 word = [
                     inc_ref[k, c, pl.ds(base + g * SUB * words + w, SUB, stride=words), :] for g in range(groups)
@@ -164,73 +180,85 @@
             )
             skim_out[k, c:c + 1, :] = summed[0:1, :]
 
-    def reduce_pair(k):
-        aon_own[k] = aon_own[k] + pair_buf[k]
-
-    def aon_sum(k):
-        total = aon_own[k, 0]
-        for j in range(1, half):
-            total = total + rs_buf[k, j]
-        aon_total[k] = total
-
     def next_flow(k):
         step = step_ref[k]
         for c in range(class_local):
             now = flow_of(k, c)
-            flows_all[k + 1, my_cls, pl.ds(c, link_rows, stride=class_local), :] = now + step * (aon_total[k, c] - now)
+            flows_all[k + 1, my_cls, pl.ds(c, link_rows, stride=class_local), :] = now + step * (aon[k, 0, 0, c] - now)
 
     def partials(k):
         cost = path = None
         for c in range(class_local):
-            value = times[k, 0, 0, c]
-            a, b = fold_rows(value * flow_of(k, c)), fold_rows(value * aon_total[k, c])
+            value = times[k, 0, c]
+            a, b = fold_rows(value * flow_of(k, c)), fold_rows(value * aon[k, 0, 0, c])
             cost = a if cost is None else cost + a
             path = b if path is None else path + b
         part_one[my_cls, 2 * k] = cost
         part_one[my_cls, 2 * k + 1] = path
 
-    flows_all[0, my_cls] = flow_ref[...]
-    aon_chunks(0, other, aon_pair)
+    def halve_first(k):
+        aon[k, 0] = aon[k, 0] + aon_recv[k, 1]
+        return {r: load_send(k, r) for r in reversed(range(2, n_org, 2)) if r & -r == 2}
+
+    def halve_next(k, sent, level):
+        for r in sorted(sent, reverse=True):
+            held = r - (r & -r)
+            if r & -r == level // 2 and held:
+                sent[r].wait()
+                load_join(k, r)
+                if held & -held == level:
+                    sent[held] = load_send(k, held)
+
+    def halve_last(k, sent):
+        for level in levels[1:]:
+            sent[level].wait()
+            load_join(k, level)
+
+    def costs_ready(k):
+        for c in range(class_local):
+            times[k, 0, c] = link_time(k, c)
+        return time_sends(k, 0)
+
+    def wait_all(group):
+        for made in group:
+            made.wait()
+
+    order = sorted(range(1, n_org), key=lambda m: (m % 2, bin(m).count("1"), m))
+    even = [m for m in order if m % 2 == 0]
+    odd = [m for m in order if m % 2 == 1]
+
+    loads[0].wait()
+    aon_chunks(0, 1)
     pl.semaphore_wait(barrier, n_org - 1 + n_cls - 1)
     pair0 = pair_copy(0)
     flow0 = flow_copies(0, flow_ref)
-    aon_chunks(0, core, aon_own)
+    flows_all[0, my_cls] = flow_ref[...]
+    aon_chunks(0, 0)
     pair0.wait()
-    reduce_pair(0)
-    rs0 = rs_copies(0)
-    for made in flow0:
-        made.wait()
-    for c in range(class_local):
-        times[0, 0, 0, c] = link_time(0, c)
-    time0 = time_copies(0)
-    aon_chunks(1, other, aon_pair)
+    sums0 = halve_first(0)
+    loads[1].wait()
+    aon_chunks(1, 1)
     pair1 = pair_copy(1)
-    aon_chunks(1, core, aon_own)
+    aon_chunks(1, 0)
+    for level in levels[2:]:
+        halve_next(0, sums0, level)
     pair1.wait()
-    reduce_pair(1)
-    rs1 = rs_copies(1)
-    skim_chunk(0, 0, 0, True)
-    for made in rs0:
-        made.wait()
-    aon_sum(0)
+    sums1 = halve_first(1)
+    inter_load.wait()
+    wait_all(flow0)
+    sent0 = costs_ready(0)
+    halve_last(0, sums0)
     next_flow(0)
     flow1 = flow_copies(1, flows_all.at[1, my_cls])
-    time0[0].wait()
-    forward0 = []
-    for j in range(1, half):
-        time0[j].wait()
-        forward0.append(forward(0, j))
-    skim_chunk(0, 0, 1, False)
-    for j in range(1, half):
-        skim_chunk(0, j, 0, False)
-    for made in flow1:
-        made.wait()
-    for c in range(class_local):
-        times[1, 0, 0, c] = link_time(1, c)
-    time1 = time_copies(1)
-    for made in rs1:
-        made.wait()
-    aon_sum(1)
+    for level in levels[2:]:
+        halve_next(1, sums1, level)
+    for m in even:
+        sent0[m].wait()
+        sent0.update(time_sends(0, m))
+    skim_chunk(0, 0)
+    wait_all(flow1)
+    sent1 = costs_ready(1)
+    halve_last(1, sums1)
     next_flow(1)
     flow2 = flow_copies(2, flows_all.at[2, my_cls])
     partials(0)
@@ -240,18 +268,15 @@
         for i in range(1, n_cls)
     ]
     flow_out[...] = flows_all[2, my_cls]
-    for j in range(1, half):
-        forward0[j - 1].wait()
-        skim_chunk(0, j, 1, False)
-    skim_finish(0)
-    skim_chunk(1, 0, 0, True)
-    time1[0].wait()
-    forward1 = []
-    for j in range(1, half):
-        time1[j].wait()
-        forward1.append(forward(1, j))
-    for made in first_sums:
-        made.wait()
+    middle = even[len(even) // 2:]
+    for m in even[:len(even) // 2]:
+        skim_chunk(0, m)
+    for m in even:
+        sent1[m].wait()
+        sent1.update(time_sends(1, m))
+        if m in middle:
+            skim_chunk(0, m)
+    wait_all(first_sums)
     total = part_one[0]
     for i in range(1, n_cls):
         total = total + part_one[i]
@@ -260,19 +285,20 @@
         copy(part_two.at[my_org], part_two.at[my_org], two_send.at[i], two_recv.at[i], {"org": (my_org + i) % n_org})
         for i in range(1, n_org)
     ]
-    skim_chunk(1, 0, 1, False)
-    for j in range(1, half):
-        skim_chunk(1, j, 0, False)
-    for made in flow2:
-        made.wait()
+    for m in odd:
+        sent0[m].wait()
+        skim_chunk(0, m)
+    skim_finish(0)
+    for m in [0] + even:
+        skim_chunk(1, m)
+    wait_all(flow2)
     for c in range(class_local):
         cost_out[pl.ds(c, link_rows, stride=class_local), :] = link_time(2, c)
-    for j in range(1, half):
-        forward1[j - 1].wait()
-        skim_chunk(1, j, 1, False)
+    for m in odd:
+        sent1[m].wait()
+        skim_chunk(1, m)
     skim_finish(1)
-    for made in second_sums:
-        made.wait()
+    wait_all(second_sums)
     total = part_two[0]
     for i in range(1, n_org):
         total = total + part_two[i]
@@ -285,13 +311,18 @@
     gap_out[...] = gaps[:, :iters]
 
 
+def hand_over(*refs):
+    count = len(refs) // 2
+    for source, target in zip(refs[:count], refs[count:]):
+        target[...] = source[...]
+
+
 def shards(n_cls, n_org, flows_start, interaction, free_time, capacity, demand, incidence, step_size):
     class_local, link_shard = flows_start.shape
     class_count = interaction.shape[1]
     iters, _, anchors, words, links = incidence.shape
     assert iters == 2 and anchors == 1 and class_count == n_cls * class_local
     link_rows = link_shard // LANES
-    half = n_org // 2
 
     def interleave(x):
         lead = x.shape[:-2]
@@ -305,6 +336,7 @@
 
     inc = interleave(incidence.reshape(iters, class_local, words, links))
     vmem = pl.BlockSpec(memory_space=pltpu.VMEM)
+    hbm = pl.BlockSpec(memory_space=pl.ANY)
     smem = pl.BlockSpec(memory_space=pltpu.SMEM)
     f32 = jnp.float32
     tile = (class_local, link_rows, LANES)
@@ -318,24 +350,23 @@
             jax.ShapeDtypeStruct((iters, class_local, count), f32),
             jax.ShapeDtypeStruct((1, iters), f32),
         ),
-        in_specs=[vmem] * 6 + [smem],
+        in_specs=[vmem, hbm, vmem, vmem, vmem, hbm, smem],
         out_specs=(vmem,) * 4,
         scratch_shapes=[
+            pltpu.VMEM((iters, class_local, words * links // LANES, LANES), jnp.int32),
+            pltpu.VMEM((class_local, class_count * link_rows, LANES), f32),
             pltpu.VMEM((iters + 1, n_cls, class_local * link_rows, LANES), f32),
-            pltpu.VMEM((iters, half) + tile, f32),
-            pltpu.VMEM((iters, half) + tile, f32),
-            pltpu.VMEM((iters, half) + tile, f32),
-            pltpu.VMEM((iters, half) + tile, f32),
-            pltpu.VMEM((iters,) + tile, f32),
-            pltpu.VMEM((iters, half, 2) + tile, f32),
+            pltpu.VMEM((iters, 2, n_org // 2) + tile, f32),
+            pltpu.VMEM((iters, 2, n_org // 2) + tile, f32),
+            pltpu.VMEM((iters, n_org) + tile, f32),
             pltpu.VMEM((iters, class_local, words * BITS * SUB, LANES), f32),
             pltpu.VMEM((n_cls, 2 * iters, SUB, LANES), f32),
             pltpu.VMEM((n_org, 2 * iters, SUB, LANES), f32),
+            dma((iters,)), dma,
             dma((iters + 1, n_cls)), dma((iters + 1, n_cls)),
             dma((iters,)), dma((iters,)),
-            dma((iters, half)), dma((iters, half)),
-            dma((iters, half)), dma((iters, half)),
-            dma((iters, half)), dma((iters, half)),
+            dma((iters, n_org)), dma((iters, n_org)),
+            dma((iters, n_org)), dma((iters, n_org)),
             dma((n_cls,)), dma((n_cls,)),
             dma((n_org,)), dma((n_org,)),
         ],
@@ -344,7 +375,12 @@
         interleave(flows_start), interleave(interaction), interleave(free_time),
         capacity.reshape(link_rows, LANES), demand.reshape(class_local, count), inc, step_size,
     )
-    flows, costs, skims, gaps = outs
+    flows, costs, skims, gaps = pl.pallas_call(
+        hand_over,
+        out_shape=tuple(jax.ShapeDtypeStruct(x.shape, x.dtype) for x in outs),
+        in_specs=[vmem] * len(outs),
+        out_specs=(vmem,) * len(outs),
+    )(*outs)
     return restore(flows), restore(costs), skims.reshape(iters, class_local, anchors, count), gaps.reshape(iters)
 
 

time: 40.4 us -> 38.1 us (0.943)
  local copies, waits for them, and re-layouts: 5.21 us -> 0 us
  Pallas kernels: 34.2 us -> 37.2 us
    unnamed x4 -> x0, local copies, waits for them, and re-layouts: 5.21 us -> none
    pallas_call x1, Pallas kernels: 34.2 us -> 35.7 us  [shards(): pl.pallas_call(functools.partial(kernel, n_cls, n_org, iters, class_local...]
    pallas_call x0 -> x1, Pallas kernels: none -> 1.47 us  [shards(): pl.pallas_call(hand_over, out_shape=tuple((jax.ShapeDtypeStruct(x.shape,...]
where the time goes in v2:
time: 38.1 us; the launch traced here: 37.8 us
  Pallas kernels  37.2 us (98%)
  between operations  0.64 us (2%)
    pallas_call x1, Pallas kernels, shards(): pl.pallas_call(functools.partial(kernel, n_cls, n_org, iters, class_local...  35.7 us
    pallas_call x1, Pallas kernels, shards(): pl.pallas_call(hand_over, out_shape=tuple((jax.ShapeDtypeStruct(x.shape,...  1.47 us

profile of v2, /device:TPU:0, one launch (start us, length us, event | category | flops | bytes accessed | tf_op | source)
XLA Modules:
  0.0 37.8 jit_solution(5574559827504297246)
XLA Ops:
  0.6 35.7 %shard_map.102 = (f32[96,128]{1,0:T(8,128)}, f32[96,128]{1,0:T(8,128)}, f32[2,2,60]{2,1,0:T(2,128)}, f32[1,2]{1,0:T(1,128)}) custom-call(f32[96,128]{1,0:T(8,128)} %bitcast.38, f32[2,384,128]{2,1,0:T(8,128)} %bitcast.37, f32[96,128]{1,0:T(8,128)} %bitcast.39, f32[48,128]{1,0:T(8,128)} %bitcast.40, s32[2,60]{1,0:T(2,128)} %bitcast.41, ...), custom_call_target="tpu_custom_call" | custom-call | tf_op jit(solution)/shard_map/pallas_call | solution.py:345
  36.3 1.5 %shard_map.103 = (f32[96,128]{1,0:T(8,128)}, f32[96,128]{1,0:T(8,128)}, f32[2,2,60]{2,1,0:T(2,128)}, f32[1,2]{1,0:T(1,128)}) custom-call(f32[96,128]{1,0:T(8,128)} %get-tuple-element.12.refs_0_, f32[96,128]{1,0:T(8,128)} %get-tuple-element.13.refs_1_, f32[2,2,60]{2,1,0:T(2,128)} %get-tuple-element.14.refs_2_, f32[1,2]{1,0:T(1,128)} %get-tuple-element.15.refs_3_), custom_call_target="tpu_custom_call" | custom-call | tf_op jit(solution)/shard_map/pallas_call | solution.py:378
